TPU v7x, 256 devices: a whole 4x4x8 slice. The times are simulated.
256 devices in a mesh: wide: 64 (over y, z, x_hi), narrow: 4 (over x_lo, core).
Axes of the slice: x: 4 (x_hi: 2, x_lo: 2; x = x_hi * 2 + x_lo), y: 4, z: 8, core: 2. Of those that a mesh axis runs over, the one named last changes fastest.
Arguments:
- rhs: float32 [3, 256, 32, 128], P(None, 'wide', 'narrow'), may hold values from -12 to 12
- start: float32 [3, 256, 32, 128], P(None, 'wide', 'narrow'), may hold values from -2 to 2
- trans: float32 [3, 256, 32, 128], P(None, 'wide', 'narrow'), may hold values from 0.2 to 2
- accum: float32 [256, 32, 128], P('wide', 'narrow'), may hold values from 2 to 8
- coupling: float32 [3, 3, 256, 32, 128], P(None, None, 'wide', 'narrow'), may hold values from -0.3 to 0.3
- well_cells: int32 [64, 4, 64], P('wide', 'narrow'), may hold values from 0 to 4095
- well_index: float32 [64, 4, 64], P('wide', 'narrow'), may hold values from 1 to 20
- agg_map: int32 [256, 32, 128], P('wide', 'narrow'), may hold values from 0 to 31
- tile_factors: bfloat16 [384, 48, 128, 128], P('wide', 'narrow')
- coarse_inverse: float32 [8192, 8192], P(('wide', 'narrow')), as said below
Outputs:
- iterate: float32 [3, 256, 32, 128], P(None, 'wide', 'narrow')
- residual: float32 [3, 256, 32, 128], P(None, 'wide', 'narrow')
Inputs may be any that keep to these rules, and one draw needn't show every extreme that they name: well_cells names, for each device's 64 connections, one of that device's own 4 * 8 * 128 cells, counted by pair, then column, then position in the tile; connections may share a cell. agg_map names one of the 32 aggregates of the device that owns the cell. coarse_inverse is symmetric.
All inputs are finite; a program needn't handle non-finite values.
Results may differ from a plain program's by a relative error of at most 0.00095.
Values sent between devices are 32-bit elements; how exact they have to be, the bound alone decides.
A program may use at most 64 MiB of HBM per device.

v0:
```python
import jax
import jax.numpy as jnp
from jax import lax
from jax.sharding import PartitionSpec as P

AGG_LOC = 32
SWEEPS = 3
INNER = 3


best_precision = lax.Precision.HIGHEST


def padded(cells, sides, width):
    for axis, dim in sides:
        count = lax.axis_size(axis)
        head = lax.slice_in_dim(cells, 0, width, axis=dim)
        tail = lax.slice_in_dim(cells, cells.shape[dim] - width, cells.shape[dim], axis=dim)
        cells = jnp.concatenate(
            [
                lax.ppermute(tail, axis, [(i, (i + 1) % count) for i in range(count)]),
                cells,
                lax.ppermute(head, axis, [((i + 1) % count, i) for i in range(count)]),
            ],
            axis=dim,
        )
    return cells


def neighbour(values, along, offset):
    along = along % values.ndim
    length = values.shape[along]
    padding = [(0, 0)] * values.ndim
    if offset > 0:
        padding[along] = (0, offset)
        return lax.slice_in_dim(jnp.pad(values, padding), offset, offset + length, axis=along)
    padding[along] = (-offset, 0)
    return lax.slice_in_dim(jnp.pad(values, padding), 0, length, axis=along)


def east_of(values):
    middle = values.shape[-1] // 2
    from_next = neighbour(values, -3, 1)[..., :middle]
    return jnp.concatenate([values[..., middle:], from_next], axis=-1)


def west_of(values):
    middle = values.shape[-1] // 2
    from_prev = neighbour(values, -3, -1)[..., middle:]
    return jnp.concatenate([from_prev, values[..., :middle]], axis=-1)


def prepare(trans, accum_w):
    middle = trans.shape[-1] // 2
    layer_no = lax.broadcasted_iota(jnp.int32, accum_w.shape, accum_w.ndim - 1) % middle
    trans_x = trans[0]
    trans_y = trans[1]
    trans_z = jnp.where(layer_no < middle - 1, trans[2], 0.0)
    face_sum = trans_x + west_of(trans_x) + trans_y + neighbour(trans_y, -2, -1)
    face_sum = face_sum + trans_z + neighbour(trans_z, -1, -1)
    return (trans_x, trans_y, trans_z, accum_w + face_sum)


def operate(values, trans_x, trans_y, trans_z, centre, coupling):
    mixing = jnp.sum(coupling * values[None], axis=1)
    inflow = trans_x * east_of(values) + west_of(trans_x) * west_of(values)
    inflow = inflow + trans_y * neighbour(values, -2, 1)
    inflow = inflow + neighbour(trans_y, -2, -1) * neighbour(values, -2, -1)
    inflow = inflow + trans_z * neighbour(values, -1, 1)
    inflow = inflow + neighbour(trans_z, -1, -1) * neighbour(values, -1, -1)
    return centre * values + mixing - inflow


def tile_apply(values, inverse_diag, factors):
    scaled = (inverse_diag * values).astype(jnp.bfloat16)
    return jnp.einsum("cpyj,pykj->cpyk", scaled, factors, preferred_element_type=jnp.float32)


def local_solve(misfit, coeffs, inverse_diag, factors):
    trans_x, trans_y, trans_z, centre, coupling = coeffs
    update = tile_apply(misfit, inverse_diag, factors)
    for _ in range(INNER - 1):
        applied = operate(update, trans_x, trans_y, trans_z, centre, coupling)
        update = update + tile_apply(misfit - applied, inverse_diag, factors)
    return update


def per_device(
    rhs,
    start,
    trans,
    accum,
    coupling,
    well_cells,
    well_index,
    agg_map,
    tile_factors,
    coarse_inverse,
):
    phases = rhs.shape[0]
    accum_flat = accum.reshape(-1).at[well_cells.reshape(-1)].add(well_index.reshape(-1))
    accum_w = accum_flat.reshape(accum.shape)
    stacked = jnp.concatenate(
        [trans, accum_w[None], coupling.reshape((phases * phases,) + accum.shape)], axis=0
    )
    stacked = jnp.concatenate([stacked, rhs], axis=0)
    rim_wide = padded(stacked, (("wide", 1),), 2)
    rim_full = padded(rim_wide, (("narrow", 2),), 3)
    trans_x, trans_y, trans_z, centre = prepare(rim_full[0:3], rim_full[3])
    coupling_full = rim_full[4:13].reshape((phases, phases) + rim_full.shape[1:])
    full_set = (trans_x, trans_y, trans_z, centre, coupling_full)
    ext_set = tuple((member[..., 1:-1, 1:-1, :] for member in full_set))
    diag_part = jnp.stack([ext_set[4][member, member] for member in range(phases)])
    inverse_diag = 1.0 / (ext_set[3][None] + diag_part)

    def extended_fn(current):
        rim_x = padded(current, (("wide", 1),), 2)
        rim_xy = padded(rim_x, (("narrow", 2),), 3)
        applied = operate(rim_xy, full_set[0], full_set[1], full_set[2], full_set[3], full_set[4])
        extended = (rim_full[13:] - applied)[..., 1:-1, 1:-1, :]
        return (extended, extended[..., 1:-1, 2:-2, :])

    groups = jnp.arange(AGG_LOC, dtype=jnp.int32)
    member_of = (groups[:, None] == agg_map.reshape(1, -1)).astype(jnp.float32)
    current = start
    for _ in range(SWEEPS):
        extended, owned_misfit = extended_fn(current)
        coarse_rhs = jnp.dot(member_of, owned_misfit[0].reshape(-1), precision=best_precision)
        coarse_all = lax.all_gather(coarse_rhs, ("wide", "narrow"), axis=0, tiled=True)
        coarse_sol = jnp.dot(coarse_inverse, coarse_all, precision=best_precision)
        update = local_solve(extended, ext_set, inverse_diag, tile_factors)[..., 1:-1, 2:-2, :]
        lifted = jnp.dot(coarse_sol, member_of, precision=best_precision).reshape(accum.shape)
        current = current + update.at[0].add(lifted)
    final_misfit = extended_fn(current)[1]
    return (current, final_misfit)


def solution(mesh):
    return jax.shard_map(
        per_device,
        mesh=mesh,
        in_specs=(
            P(None, "wide", "narrow", None),
            P(None, "wide", "narrow", None),
            P(None, "wide", "narrow", None),
            P("wide", "narrow", None),
            P(None, None, "wide", "narrow", None),
            P("wide", "narrow", None),
            P("wide", "narrow", None),
            P("wide", "narrow", None),
            P("wide", "narrow", None, None),
            P(("wide", "narrow"), None),
        ),
        out_specs=(P(None, "wide", "narrow", None), P(None, "wide", "narrow", None)),
        check_vma=False,
    )
```

profile of v0, /device:TPU:1, one launch (start us, length us, event | category | flops | bytes accessed | tf_op | source)
XLA Modules:
  0.0 364.7 jit_solution(14993935631238737377)
XLA Ops:
  6.0 3.6 collective-permute-start
  9.7 7.8 %collective-permute-start.1 = (f32[16,2,8,128]{3,0,2,1:T(8,128)S(1)}, f32[16,2,8,128]{3,0,2,1:T(8,128)S(1)}, u32[]{:S(2)}, u32[]{:S(2)}) collective-permute-start(f32[16,2,8,128]{3,0,2,1:T(8,128)S(1)} %get-tuple-element.65), channel_id=1, source_target_pairs={{4,0},{8,4},{12,8},{16,12},{20,16},{24,20},{28,24},{32,28},{36,32}... | collective-permute-start | bytes 393224 | tf_op jit(solution)/shard_map/ppermute | solution.py:23
  17.7 7.2 %collective-permute-start.5 = (f32[3,2,8,128]{3,0,2,1:T(4,128)S(1)}, f32[3,2,8,128]{3,0,2,1:T(4,128)S(1)}, u32[]{:S(2)}, u32[]{:S(2)}) collective-permute-start(f32[3,2,8,128]{3,0,2,1:T(4,128)S(1)} %copy.305), channel_id=1, source_target_pairs={{4,0},{8,4},{12,8},{16,12},{20,16},{24,20},{28,24},{32,28},{36,32}... | collective-permute-start | bytes 73736 | tf_op jit(solution)/shard_map/ppermute | solution.py:23
  26.9 2.3 collective-permute-start.6
  30.7 2.2 collective-permute-done.7
  34.1 1.8 collective-permute-done.2
  35.9 3.7 %collective-permute-done.3 = f32[16,8,3,128]{3,0,2,1:T(8,128)S(1)} collective-permute-done((f32[16,8,3,128]{3,0,2,1:T(8,128)S(1)}, f32[16,8,3,128]{3,0,2,1:T(8,128)S(1)}, u32[]{:S(2)}, u32[]{:S(2)}) %collective-permute-start.3) | collective-permute-done | bytes 196640 | tf_op jit(solution)/shard_map/ppermute | solution.py:23
  50.0 77.4 %all-reduce.66 = f32[8192]{0:T(1024)} all-reduce(f32[8192]{0:T(1024)} %dynamic-update-slice.9), channel_id=1, replica_groups=mesh['wide'=64,'narrow'=4] {'wide','narrow'}, use_global_device_ids=true, to_apply=%add.66 | all-reduce | flops 8192 | bytes 65536
  127.5 2.2 convolution_bitcast_fusion.11
  129.9 2.7 fusion.4
  134.9 6.0 %collective-permute-start.9 = (f32[3,2,8,128]{3,0,2,1:T(4,128)S(1)}, f32[3,2,8,128]{3,0,2,1:T(4,128)S(1)}, u32[]{:S(2)}, u32[]{:S(2)}) collective-permute-start(f32[3,2,8,128]{3,0,2,1:T(4,128)S(1)} %get-tuple-element.123), channel_id=1, source_target_pairs={{4,0},{8,4},{12,8},{16,12},{20,16},{24,20},{28,24},{32,28},{36,32}... | collective-permute-start | bytes 73736 | tf_op jit(solution)/shard_map/ppermute | solution.py:23
  145.1 2.4 collective-permute-done.11
  148.0 1.7 fusion.29
  157.1 78.3 %all-reduce.67 = f32[8192]{0:T(1024)} all-reduce(f32[8192]{0:T(1024)} %dynamic-update-slice.10), channel_id=1, replica_groups=mesh['wide'=64,'narrow'=4] {'wide','narrow'}, use_global_device_ids=true, to_apply=%add.67 | all-reduce | flops 8192 | bytes 65536
  235.4 2.2 convolution_bitcast_fusion.10
  238.6 2.7 fusion.2
  242.7 6.0 %collective-permute-start.13 = (f32[3,2,8,128]{3,0,2,1:T(4,128)S(1)}, f32[3,2,8,128]{3,0,2,1:T(4,128)S(1)}, u32[]{:S(2)}, u32[]{:S(2)}) collective-permute-start(f32[3,2,8,128]{3,0,2,1:T(4,128)S(1)} %get-tuple-element.121), channel_id=1, source_target_pairs={{4,0},{8,4},{12,8},{16,12},{20,16},{24,20},{28,24},{32,28},{36,32}... | collective-permute-start | bytes 73736 | tf_op jit(solution)/shard_map/ppermute | solution.py:23
  250.7 2.0 collective-permute-start.15
  254.9 1.7 fusion.37
  264.0 79.4 %all-reduce.68 = f32[8192]{0:T(1024)} all-reduce(f32[8192]{0:T(1024)} %dynamic-update-slice.11), channel_id=1, replica_groups=mesh['wide'=64,'narrow'=4] {'wide','narrow'}, use_global_device_ids=true, to_apply=%add.68 | all-reduce | flops 8192 | bytes 65536
  343.4 2.2 convolution_bitcast_fusion.9
  345.9 2.7 fusion
  350.0 6.0 %collective-permute-start.17 = (f32[3,2,8,128]{3,0,2,1:T(4,128)S(1)}, f32[3,2,8,128]{3,0,2,1:T(4,128)S(1)}, u32[]{:S(2)}, u32[]{:S(2)}) collective-permute-start(f32[3,2,8,128]{3,0,2,1:T(4,128)S(1)} %get-tuple-element.119), channel_id=1, source_target_pairs={{4,0},{8,4},{12,8},{16,12},{20,16},{24,20},{28,24},{32,28},{36,32}... | collective-permute-start | bytes 73736 | tf_op jit(solution)/shard_map/ppermute | solution.py:23
  358.0 1.8 collective-permute-start.19
  (247 shorter events, 56.6 us)
Async XLA Ops:
  0.6 41.6 %copy-start = (bf16[6,12,128,128]{3,2,1,0:T(8,128)(2,1)S(1)}, bf16[6,12,128,128]{3,2,1,0:T(8,128)(2,1)}, u32[]{:S(2)}) copy-start(bf16[6,12,128,128]{3,2,1,0:T(8,128)(2,1)} %param.24) | copy-start | bytes 7077892
  6.0 26.9 %collective-permute-start = (f32[16,2,8,128]{3,0,2,1:T(8,128)S(1)}, f32[16,2,8,128]{3,0,2,1:T(8,128)S(1)}, u32[]{:S(2)}, u32[]{:S(2)}) collective-permute-start(f32[16,2,8,128]{3,0,2,1:T(8,128)S(1)} %get-tuple-element.64), channel_id=1, source_target_pairs={{0,4},{4,8},{8,12},{12,16},{16,20},{20,24},{24,28},{28,32},{32,36}... | collective-permute-start | bytes 393224 | tf_op jit(solution)/shard_map/ppermute | solution.py:21
  9.7 23.3 %collective-permute-start.1 = (f32[16,2,8,128]{3,0,2,1:T(8,128)S(1)}, f32[16,2,8,128]{3,0,2,1:T(8,128)S(1)}, u32[]{:S(2)}, u32[]{:S(2)}) collective-permute-start(f32[16,2,8,128]{3,0,2,1:T(8,128)S(1)} %get-tuple-element.65), channel_id=1, source_target_pairs={{4,0},{8,4},{12,8},{16,12},{20,16},{24,20},{28,24},{32,28},{36,32}... | collective-permute-start | bytes 393224 | tf_op jit(solution)/shard_map/ppermute | solution.py:23
  17.6 8.6 %collective-permute-start.4 = (f32[3,2,8,128]{3,0,2,1:T(4,128)S(1)}, f32[3,2,8,128]{3,0,2,1:T(4,128)S(1)}, u32[]{:S(2)}, u32[]{:S(2)}) collective-permute-start(f32[3,2,8,128]{3,0,2,1:T(4,128)S(1)} %copy.304), channel_id=1, source_target_pairs={{0,4},{4,8},{8,12},{12,16},{16,20},{20,24},{24,28},{28,32},{32,36}... | collective-permute-start | bytes 73736 | tf_op jit(solution)/shard_map/ppermute | solution.py:21
  17.7 8.5 %collective-permute-start.5 = (f32[3,2,8,128]{3,0,2,1:T(4,128)S(1)}, f32[3,2,8,128]{3,0,2,1:T(4,128)S(1)}, u32[]{:S(2)}, u32[]{:S(2)}) collective-permute-start(f32[3,2,8,128]{3,0,2,1:T(4,128)S(1)} %copy.305), channel_id=1, source_target_pairs={{4,0},{8,4},{12,8},{16,12},{20,16},{24,20},{28,24},{32,28},{36,32}... | collective-permute-start | bytes 73736 | tf_op jit(solution)/shard_map/ppermute | solution.py:23
  26.9 3.8 %collective-permute-start.6 = (f32[3,8,3,128]{3,0,2,1:T(4,128)}, f32[3,8,3,128]{3,0,2,1:T(4,128)S(1)}, u32[]{:S(2)}, u32[]{:S(2)}) collective-permute-start(f32[3,8,3,128]{3,0,2,1:T(4,128)} %get-tuple-element.116), channel_id=1, source_target_pairs={{0,1},{1,2},{2,3},{3,0},{4,5},{5,6},{6,7},{7,4},{8,9},{9,10},{10,1... | collective-permute-start | bytes 110600 | tf_op jit(solution)/shard_map/ppermute | solution.py:21
  29.2 3.7 %collective-permute-start.7 = (f32[3,8,3,128]{3,0,2,1:T(4,128)}, f32[3,8,3,128]{3,0,2,1:T(4,128)S(1)}, u32[]{:S(2)}, u32[]{:S(2)}) collective-permute-start(f32[3,8,3,128]{3,0,2,1:T(4,128)} %get-tuple-element.117), channel_id=1, source_target_pairs={{1,0},{2,1},{3,2},{0,3},{5,4},{6,5},{7,6},{4,7},{9,8},{10,9},{11,1... | collective-permute-start | bytes 110600 | tf_op jit(solution)/shard_map/ppermute | solution.py:23
  33.1 2.8 collective-permute-start.2
  33.2 6.3 %collective-permute-start.3 = (f32[16,8,3,128]{3,0,2,1:T(8,128)S(1)}, f32[16,8,3,128]{3,0,2,1:T(8,128)S(1)}, u32[]{:S(2)}, u32[]{:S(2)}) collective-permute-start(f32[16,8,3,128]{3,0,2,1:T(8,128)S(1)} %get-tuple-element.60), channel_id=1, source_target_pairs={{1,0},{2,1},{3,2},{0,3},{5,4},{6,5},{7,6},{4,7},{9,8},{10,9},{11,1... | collective-permute-start | bytes 589832 | tf_op jit(solution)/shard_map/ppermute | solution.py:23
  40.3 107.6 %copy-start.2 = (f32[8,14,128]{2,1,0:T(8,128)}, f32[8,14,128]{2,1,0:T(8,128)S(1)}, u32[]{:S(2)}) copy-start(f32[8,14,128]{2,1,0:T(8,128)S(1)} %get-tuple-element.130) | copy-start | bytes 172036
  40.8 89.2 %copy-start.4 = (f32[6,12,128]{2,1,0:T(8,128)}, f32[6,12,128]{2,1,0:T(8,128)S(1)}, u32[]{:S(2)}) copy-start(f32[6,12,128]{2,1,0:T(8,128)S(1)} %copy.186) | copy-start | bytes 110596
  133.6 8.6 %collective-permute-start.8 = (f32[3,2,8,128]{3,0,2,1:T(4,128)S(1)}, f32[3,2,8,128]{3,0,2,1:T(4,128)S(1)}, u32[]{:S(2)}, u32[]{:S(2)}) collective-permute-start(f32[3,2,8,128]{3,0,2,1:T(4,128)S(1)} %get-tuple-element.122), channel_id=1, source_target_pairs={{0,4},{4,8},{8,12},{12,16},{16,20},{20,24},{24,28},{28,32},{32,36}... | collective-permute-start | bytes 73736 | tf_op jit(solution)/shard_map/ppermute | solution.py:21
  134.9 7.3 %collective-permute-start.9 = (f32[3,2,8,128]{3,0,2,1:T(4,128)S(1)}, f32[3,2,8,128]{3,0,2,1:T(4,128)S(1)}, u32[]{:S(2)}, u32[]{:S(2)}) collective-permute-start(f32[3,2,8,128]{3,0,2,1:T(4,128)S(1)} %get-tuple-element.123), channel_id=1, source_target_pairs={{4,0},{8,4},{12,8},{16,12},{20,16},{24,20},{28,24},{32,28},{36,32}... | collective-permute-start | bytes 73736 | tf_op jit(solution)/shard_map/ppermute | solution.py:23
  142.2 2.9 collective-permute-start.10
  143.2 4.3 %collective-permute-start.11 = (f32[3,8,3,128]{3,0,2,1:T(4,128)S(1)}, f32[3,8,3,128]{3,0,2,1:T(4,128)S(1)}, u32[]{:S(2)}, u32[]{:S(2)}) collective-permute-start(f32[3,8,3,128]{3,0,2,1:T(4,128)S(1)} %get-tuple-element.115), channel_id=1, source_target_pairs={{1,0},{2,1},{3,2},{0,3},{5,4},{6,5},{7,6},{4,7},{9,8},{10,9},{11,1... | collective-permute-start | bytes 110600 | tf_op jit(solution)/shard_map/ppermute | solution.py:23
  152.9 85.7 %copy-start.6 = (f32[6,12,128]{2,1,0:T(8,128)S(1)}, f32[6,12,128]{2,1,0:T(8,128)}, u32[]{:S(2)}) copy-start(f32[6,12,128]{2,1,0:T(8,128)} %copy-done.4) | copy-start | bytes 110596
  241.4 8.6 %collective-permute-start.12 = (f32[3,2,8,128]{3,0,2,1:T(4,128)S(1)}, f32[3,2,8,128]{3,0,2,1:T(4,128)S(1)}, u32[]{:S(2)}, u32[]{:S(2)}) collective-permute-start(f32[3,2,8,128]{3,0,2,1:T(4,128)S(1)} %get-tuple-element.120), channel_id=1, source_target_pairs={{0,4},{4,8},{8,12},{12,16},{16,20},{20,24},{24,28},{28,32},{32,36}... | collective-permute-start | bytes 73736 | tf_op jit(solution)/shard_map/ppermute | solution.py:21
  242.7 7.3 %collective-permute-start.13 = (f32[3,2,8,128]{3,0,2,1:T(4,128)S(1)}, f32[3,2,8,128]{3,0,2,1:T(4,128)S(1)}, u32[]{:S(2)}, u32[]{:S(2)}) collective-permute-start(f32[3,2,8,128]{3,0,2,1:T(4,128)S(1)} %get-tuple-element.121), channel_id=1, source_target_pairs={{4,0},{8,4},{12,8},{16,12},{20,16},{24,20},{28,24},{32,28},{36,32}... | collective-permute-start | bytes 73736 | tf_op jit(solution)/shard_map/ppermute | solution.py:23
  250.0 3.1 collective-permute-start.14
  250.7 3.7 %collective-permute-start.15 = (f32[3,8,3,128]{3,0,2,1:T(4,128)S(1)}, f32[3,8,3,128]{3,0,2,1:T(4,128)S(1)}, u32[]{:S(2)}, u32[]{:S(2)}) collective-permute-start(f32[3,8,3,128]{3,0,2,1:T(4,128)S(1)} %get-tuple-element.113), channel_id=1, source_target_pairs={{1,0},{2,1},{3,2},{0,3},{5,4},{6,5},{7,6},{4,7},{9,8},{10,9},{11,1... | collective-permute-start | bytes 110600 | tf_op jit(solution)/shard_map/ppermute | solution.py:23
  348.8 8.6 %collective-permute-start.16 = (f32[3,2,8,128]{3,0,2,1:T(4,128)S(1)}, f32[3,2,8,128]{3,0,2,1:T(4,128)S(1)}, u32[]{:S(2)}, u32[]{:S(2)}) collective-permute-start(f32[3,2,8,128]{3,0,2,1:T(4,128)S(1)} %get-tuple-element.118), channel_id=1, source_target_pairs={{0,4},{4,8},{8,12},{12,16},{16,20},{20,24},{24,28},{28,32},{32,36}... | collective-permute-start | bytes 73736 | tf_op jit(solution)/shard_map/ppermute | solution.py:21
  350.0 7.3 %collective-permute-start.17 = (f32[3,2,8,128]{3,0,2,1:T(4,128)S(1)}, f32[3,2,8,128]{3,0,2,1:T(4,128)S(1)}, u32[]{:S(2)}, u32[]{:S(2)}) collective-permute-start(f32[3,2,8,128]{3,0,2,1:T(4,128)S(1)} %get-tuple-element.119), channel_id=1, source_target_pairs={{4,0},{8,4},{12,8},{16,12},{20,16},{24,20},{28,24},{32,28},{36,32}... | collective-permute-start | bytes 73736 | tf_op jit(solution)/shard_map/ppermute | solution.py:23
  357.4 3.9 %collective-permute-start.18 = (f32[3,8,3,128]{3,0,2,1:T(4,128)S(1)}, f32[3,8,3,128]{3,0,2,1:T(4,128)S(1)}, u32[]{:S(2)}, u32[]{:S(2)}) collective-permute-start(f32[3,8,3,128]{3,0,2,1:T(4,128)S(1)} %get-tuple-element.110), channel_id=1, source_target_pairs={{0,1},{1,2},{2,3},{3,0},{4,5},{5,6},{6,7},{7,4},{8,9},{9,10},{10,1... | collective-permute-start | bytes 110600 | tf_op jit(solution)/shard_map/ppermute | solution.py:21
  358.0 3.5 collective-permute-start.19
  (38 other events, 112.2 us)
where the time goes:
time: 372 us; the launch traced here: 365 us
  blocking collectives  235 us (63%)
  starting transfers between devices  51.3 us (14%)
  matrix products  25.2 us (7%)
  local copies, waits for them, and re-layouts  19.3 us (5%)
  waiting for transfers between devices  19.1 us (5%)
  other arithmetic  12.4 us (3%)
    unnamed x3, blocking collectives  235 us
    ppermute x10, starting transfers between devices, padded(): lax.ppermute(head, axis, [((i + 1) % count, i) for i in range(count)])  39 us
    dot_general x9, matrix products, tile_apply(): jnp.einsum('cpyj,pykj->cpyk', scaled, factors, preferred_element_type=jnp...  16.1 us
    ppermute x10, starting transfers between devices, padded(): lax.ppermute(tail, axis, [(i, (i + 1) % count) for i in range(count)])  12.4 us
    unnamed x100, local copies, waits for them, and re-layouts  10.3 us
    ppermute x10, waiting for transfers between devices, padded(): lax.ppermute(head, axis, [((i + 1) % count, i) for i in range(count)])  9.95 us
    ppermute x10, waiting for transfers between devices, padded(): lax.ppermute(tail, axis, [(i, (i + 1) % count) for i in range(count)])  9.15 us
  transfers between devices with their start and end apart: 20, of which 13 were waited for; matrix products, arithmetic and copies ran while one was open for 1% of the time, Pallas kernels for 0%

commit v1 on v0

v1 whole, which is shorter than its diff:
```python
import functools

import jax
import jax.numpy as jnp
from jax import lax
from jax.experimental import pallas as pl
from jax.experimental.pallas import tpu as pltpu
from jax.sharding import PartitionSpec as P

GY, GZ, GX = 4, 8, 2
SWEEPS = 3
INNER = 3
AGG = 32
PX, CY, TILE = 4, 8, 128
ROW0 = 5
WIN = 16
MESH = pl.DeviceIdType.MESH
F32 = jnp.float32
BF16 = jnp.bfloat16

DIRS = [(1, 0), (-1, 0), (0, 1), (0, -1), (1, 1), (1, -1), (-1, 1), (-1, -1)]


def span(step, own, base, rim):
    if step > 0:
        return (base + own - rim, rim), (base - rim, rim)
    if step < 0:
        return (base, rim), (base + own, rim)
    return (base, own), (base, own)


def half_swap(v):
    return pltpu.roll(v, 64, 1)


def kernel(
    sizes, cells, wells, rhs, start, trans, accum, coupling, agg, factors, inverse, out_it, out_res,
    cur, trn, blk, aggx, fac, fct, cinv, cof, own, idx, mis, upd, ybuf, zrec, tbuf, prec, outb,
    lsem, bsem, gsend, grecv, hsend, hrecv, zsend, zrecv, psend, precv,
):
    n_wide, n_narrow = sizes
    i = lax.axis_index("wide")
    j = lax.axis_index("narrow")
    y, z, xh = i // (GZ * GX), lax.rem(i // GX, GZ), lax.rem(i, GX)

    def dev(a, b):
        return {"wide": lax.rem(i + a + n_wide, n_wide), "narrow": lax.rem(j + b + n_narrow, n_narrow)}

    def plane(dy, dx, dj):
        yy, xx = lax.rem(y + dy, GY), lax.rem(xh + dx, GX)
        return yy, xx, {"wide": (yy * GZ + z) * GX + xx, "narrow": lax.rem(j + dj, n_narrow)}

    def ring(dz):
        zz = lax.rem(z + dz, GZ)
        return zz, {"wide": (y * GZ + zz) * GX + xh, "narrow": j}

    zoff = sorted(range(1, GZ), key=lambda d: -min(d, GZ - d))
    poff = [(a, b, c) for a in range(GY) for b in range(GX) for c in range(n_narrow) if a or b or c]
    far = lambda d, n: min(d, n - d)
    porder = sorted(range(len(poff)), key=lambda s: -(far(poff[s][0], GY) + 2 * poff[s][1] + far(poff[s][2], n_narrow)))

    bar = pltpu.get_barrier_semaphore()
    peers = [ring(d)[1] for d in zoff] + [plane(*poff[s])[2] for s in porder] + [dev(a, b) for a, b in DIRS if a]
    for p in peers:
        pl.semaphore_signal(bar, inc=1, device_id=p, device_id_type=MESH)

    def load(src, dst, n):
        cp = pltpu.make_async_copy(src, dst, lsem.at[n])
        cp.start()
        return cp

    op, orow = pl.ds(2, PX), pl.ds(8, CY)
    loads = [
        load(start, cur.at[0, :, op, orow], 0),
        load(trans, trn.at[:, op, orow], 1),
        load(accum, blk.at[0, op, orow], 2),
        load(coupling, blk.at[pl.ds(1, 9), op, orow], 3),
        load(rhs, blk.at[pl.ds(10, 3), op, orow], 4),
        load(agg, aggx.at[op, orow], 5),
    ]
    load_c = load(inverse, cinv, 6)
    load_f = load(factors, fac, 7)
    upd[...] = jnp.zeros_like(upd)
    for cp in loads:
        cp.wait()

    base = lax.broadcasted_iota(jnp.int32, (PX, CY, TILE), 0) * (CY * TILE)
    base = base + lax.broadcasted_iota(jnp.int32, (PX, CY, TILE), 1) * TILE
    base = base + lax.broadcasted_iota(jnp.int32, (PX, CY, TILE), 2)

    def well(n, a):
        return a + jnp.where(base == cells[n], wells[n], 0.0)

    blk[0, 2:6, 8:16] = lax.fori_loop(0, cells.shape[0], well, blk[0, 2:6, 8:16])

    pl.semaphore_wait(bar, len(peers))

    def halo(ref, lead, rim, ssem, rsem):
        out = []
        for n, (a, b) in enumerate(DIRS):
            sp, dp = span(a, PX, 2, rim[0])
            sr, dr = span(b, CY, 8, rim[1])
            out.append(
                pltpu.make_async_remote_copy(
                    src_ref=ref.at[(*lead, pl.ds(*sp), pl.ds(*sr))],
                    dst_ref=ref.at[(*lead, pl.ds(*dp), pl.ds(*dr))],
                    send_sem=ssem.at[n],
                    recv_sem=rsem.at[n],
                    device_id=dev(a, b),
                    device_id_type=MESH,
                )
            )
        return out

    every = slice(None)
    h_cur = halo(cur, (0, every), (2, 3), gsend.at[0], grecv.at[0])
    h_trn = halo(trn, (every,), (2, 3), gsend.at[1], grecv.at[1])
    h_blk = halo(blk, (every,), (1, 2), gsend.at[2], grecv.at[2])
    h_agg = halo(aggx, (), (2, 3), gsend.at[3], grecv.at[3])
    for group in (h_cur, h_trn, h_blk, h_agg):
        for cp in group:
            cp.start()

    load_f.wait()

    def flip(t, c):
        fct[pl.ds(pl.multiple_of(t * TILE, TILE), TILE), :] = fac[t].T
        return c

    lax.fori_loop(0, fac.shape[0], flip, 0)
    load_c.wait()

    lane8 = lax.broadcasted_iota(jnp.int32, (CY, TILE), 1)
    lane16 = lax.broadcasted_iota(jnp.int32, (WIN, TILE), 1)
    row16 = lax.broadcasted_iota(jnp.int32, (WIN, TILE), 0)

    for cp in h_cur + h_trn:
        cp.wait_recv()

    for p in range(PX):
        tx, ty = trn[0, 2 + p, 8:16], trn[1, 2 + p, 8:16]
        txw = jnp.where(lane8 < 64, half_swap(trn[0, 1 + p, 8:16]), half_swap(tx))
        tz = jnp.where(lax.rem(lane8, 64) < 63, trn[2, 2 + p, 8:16], 0.0)
        tzm = pltpu.roll(tz, 1, 1)
        own[0, p], own[1, p], own[2, p] = txw, tz, tzm
        own[3, p] = blk[0, 2 + p, 8:16] + (tx + txw + ty + trn[1, 2 + p, 7:15] + tz + tzm)

    def flux(v, c, p, lo, n, lane, tx, txw, ty, tym, tz, tzm, lead):
        here = v[(*lead, c, p, pl.ds(lo, n))]
        mid = half_swap(here)
        east = jnp.where(lane < 64, mid, half_swap(v[(*lead, c, p + 1, pl.ds(lo, n))]))
        west = jnp.where(lane < 64, half_swap(v[(*lead, c, p - 1, pl.ds(lo, n))]), mid)
        total = tx * east + txw * west
        total = total + ty * v[(*lead, c, p, pl.ds(lo + 1, n))] + tym * v[(*lead, c, p, pl.ds(lo - 1, n))]
        return here, total + tz * pltpu.roll(here, TILE - 1, 1) + tzm * pltpu.roll(here, 1, 1)

    def own_misfit(k, comps, p):
        tx, ty, tym = trn[0, 2 + p, 8:16], trn[1, 2 + p, 8:16], trn[1, 2 + p, 7:15]
        txw, tz, tzm, ctr = own[0, p], own[1, p], own[2, p], own[3, p]
        res = []
        for c in comps:
            here, inflow = flux(cur, c, 2 + p, 8, CY, lane8, tx, txw, ty, tym, tz, tzm, (k,))
            mix = blk[1 + 3 * c, 2 + p, 8:16] * cur[k, 0, 2 + p, 8:16]
            for b in (1, 2):
                mix = mix + blk[1 + 3 * c + b, 2 + p, 8:16] * cur[k, b, 2 + p, 8:16]
            res.append(blk[10 + c, 2 + p, 8:16] - (ctr * here + mix - inflow))
        return res

    def prepare():
        for cp in h_blk + h_agg:
            cp.wait_recv()
        for cp in h_cur + h_trn + h_blk + h_agg:
            cp.wait_send()

        def one(p, c):
            w = pl.ds(ROW0, WIN)
            tx, ty, tym = trn[0, p, w], trn[1, p, w], trn[1, p, pl.ds(ROW0 - 1, WIN)]
            txw = jnp.where(lane16 < 64, half_swap(trn[0, p - 1, w]), half_swap(tx))
            tz = jnp.where(lax.rem(lane16, 64) < 63, trn[2, p, w], 0.0)
            tzm = pltpu.roll(tz, 1, 1)
            ctr = blk[0, p, w] + (tx + txw + ty + tym + tz + tzm)
            cof[0, p], cof[1, p], cof[2, p], cof[3, p] = txw, tz, tzm, ctr
            for b in range(3):
                cof[4 + b, p] = 1.0 / (ctr + blk[1 + 4 * b, p, w])
            return c

        lax.fori_loop(1, 7, one, 0)
        owner = jnp.where(row16 < 3, n_narrow - 1, jnp.where(row16 < 11, 0, 1)) + j
        owner = lax.rem(owner, n_narrow) * AGG
        for p in range(8):
            idx[p] = jnp.where(row16 < 14, owner + aggx[p, ROW0 : ROW0 + WIN], 0)

    def operate(v, lead, p, sub):
        w = pl.ds(ROW0, WIN)
        tx, ty, tym = trn[0, p, w], trn[1, p, w], trn[1, p, pl.ds(ROW0 - 1, WIN)]
        txw, tz, tzm, ctr = cof[0, p], cof[1, p], cof[2, p], cof[3, p]
        res = []
        for c in range(3):
            here, inflow = flux(v, c, p, ROW0, WIN, lane16, tx, txw, ty, tym, tz, tzm, lead)
            mix = blk[1 + 3 * c, p, w] * v[(*lead, 0, p, w)]
            for b in (1, 2):
                mix = mix + blk[1 + 3 * c + b, p, w] * v[(*lead, b, p, w)]
            res.append(sub(c) - (ctr * here + mix - inflow))
        return res

    def sweep(k, carry):
        m0 = [own_misfit(k, (0,), p)[0] for p in range(PX)]
        ag = [aggx[2 + p, 8:16] for p in range(PX)]
        parts = []
        for a in range(AGG):
            t = [jnp.where(ag[p] == a, m0[p], 0.0) for p in range(PX)]
            parts.append(jnp.sum((t[0] + t[1]) + (t[2] + t[3]), axis=0, keepdims=True))
        r = jnp.sum(jnp.concatenate(parts, axis=0), axis=1, keepdims=True)

        def rows(yy, c):
            for t in range(GZ * GX):
                g = pl.multiple_of((yy * (GZ * GX) + t) * TILE, TILE)
                m = cinv[:, pl.ds(g, TILE)] * r
                s = (m[0:8] + m[8:16]) + (m[16:24] + m[24:32])
                s = jnp.sum(s, axis=0, keepdims=True)
                ybuf[yy, 1 + t] = s
                if t == GZ * GX - 1:
                    ybuf[lax.rem(yy + 1, GY), 0] = s
                if t == 0:
                    ybuf[lax.rem(yy + GY - 1, GY), GZ * GX + 1] = s
            return c

        lax.fori_loop(0, GY, rows, 0)
        zcp = []
        for d in zoff:
            zz, p = ring(d)
            cp = pltpu.make_async_remote_copy(
                src_ref=ybuf.at[:, pl.ds(zz * GX, GX + 2)],
                dst_ref=zrec.at[k, d - 1],
                send_sem=zsend.at[d - 1],
                recv_sem=zrecv.at[k, d - 1],
                device_id=p,
                device_id_type=MESH,
            )
            cp.start()
            zcp.append(cp)

        pl.when(k == 0)(prepare)

        def box(p, c):
            for b, v in enumerate(operate(cur, (k,), p, lambda b: blk[10 + b, p, pl.ds(ROW0, WIN)])):
                mis[b, p] = v
            return c

        lax.fori_loop(1, 7, box, 0)
        upd[0] = jnp.zeros_like(upd[0])

        def solve(n, c):
            now = lax.rem(n, 2)

            def two(g, cc):
                for p in (1 + 2 * g, 2 + 2 * g):
                    res = operate(upd, (now,), p, lambda b: mis[b, p])
                    q = [cof[4 + b, p] * res[b] for b in range(3)]
                    cols = []
                    for t in range(CY + 4):
                        cols.append(
                            jnp.concatenate([jnp.where(row16 == t + 1, v, 0.0).astype(BF16) for v in q], axis=0)
                        )
                    lhs = jnp.concatenate(cols, axis=1)
                    depth = (CY + 4) * TILE
                    f = fct[pl.ds(pl.multiple_of((p - 1) * depth, depth), depth), :]
                    r = jnp.dot(lhs, f, preferred_element_type=F32)
                    for b in range(3):
                        w = pl.ds(ROW0, WIN)
                        upd[1 - now, b, p, w] = upd[now, b, p, w] + r[b * WIN : (b + 1) * WIN]
                return cc

            lax.fori_loop(0, 3, two, 0)
            return c

        lax.fori_loop(0, INNER, solve, 0)
        for b in range(3):
            for p in range(PX):
                cur[k + 1, b, 2 + p, 8:16] = cur[k, b, 2 + p, 8:16] + upd[INNER % 2, b, 2 + p, 8:16]
        hcp = halo(cur, (k + 1, every), (2, 3), hsend, hrecv.at[k])
        for cp in hcp:
            cp.start()

        for cp in zcp:
            cp.wait_recv()
        t = ybuf[:, pl.ds(z * GX, GX + 2)]
        for d in range(GZ - 1):
            t = t + zrec[k, d]
        tbuf[...] = t
        pcp = []
        for s in porder:
            yy, xx, p = plane(*poff[s])
            cp = pltpu.make_async_remote_copy(
                src_ref=tbuf.at[yy, pl.ds(xx, 3)],
                dst_ref=prec.at[k, s],
                send_sem=psend.at[s],
                recv_sem=precv.at[k, s],
                device_id=p,
                device_id_type=MESH,
            )
            cp.start()
            pcp.append(cp)
        for cp in zcp:
            cp.wait_send()
        for cp in hcp:
            cp.wait_send()
        for cp in hcp:
            cp.wait_recv()
        for cp in pcp:
            cp.wait_recv()
        c = tbuf[y, pl.ds(xh, 3)]
        for s in range(len(poff)):
            c = c + prec[k, s]
        for p in range(8):
            row = c[0 if p < 2 else (1 if p < 6 else 2)]
            lift = jnp.take_along_axis(
                jnp.broadcast_to(row, (WIN, TILE)), idx[p], axis=1, mode="promise_in_bounds"
            )
            cur[k + 1, 0, p, ROW0 : ROW0 + WIN] = cur[k + 1, 0, p, ROW0 : ROW0 + WIN] + lift
        for cp in pcp:
            cp.wait_send()
        return carry

    lax.fori_loop(0, SWEEPS, sweep, 0)
    for p in range(PX):
        for b, v in enumerate(own_misfit(SWEEPS, (0, 1, 2), p)):
            outb[b, p] = v
    stores = [
        load(cur.at[SWEEPS, :, op, orow], out_it, 0),
        load(outb, out_res, 1),
    ]
    for cp in stores:
        cp.wait()


def per_device(sizes, rhs, start, trans, accum, coupling, well_cells, well_index, agg_map, tile_factors, coarse_inverse):
    n_wide, n_narrow = sizes
    ext = lambda *lead: pltpu.VMEM((*lead, 8, 24, TILE), F32)
    win = lambda *lead: pltpu.VMEM((*lead, 8, WIN, TILE), F32)
    dma = pltpu.SemaphoreType.DMA
    anys = pl.BlockSpec(memory_space=pl.ANY)
    smem = pl.BlockSpec(memory_space=pltpu.SMEM)
    n_plane = GY * GX * n_narrow - 1
    shape = jax.ShapeDtypeStruct(rhs.shape, F32)
    return pl.pallas_call(
        functools.partial(kernel, sizes),
        out_shape=(shape, shape),
        in_specs=[smem, smem] + [anys] * 8,
        out_specs=(anys, anys),
        scratch_shapes=[
            ext(SWEEPS + 1, 3),
            ext(3),
            ext(13),
            pltpu.VMEM((8, 24, TILE), jnp.int32),
            pltpu.VMEM((72, TILE, TILE), BF16),
            pltpu.VMEM((72 * TILE, TILE), BF16),
            pltpu.VMEM(coarse_inverse.shape, F32),
            win(7),
            pltpu.VMEM((4, PX, CY, TILE), F32),
            pltpu.VMEM((8, WIN, TILE), jnp.int32),
            win(3),
            ext(2, 3),
            pltpu.VMEM((GY, GZ * GX + 2, 1, TILE), F32),
            pltpu.VMEM((SWEEPS, GZ - 1, GY, GX + 2, 1, TILE), F32),
            pltpu.VMEM((GY, GX + 2, 1, TILE), F32),
            pltpu.VMEM((SWEEPS, n_plane, 3, 1, TILE), F32),
            pltpu.VMEM(rhs.shape, F32),
            dma((8,)),
            dma((1,)),
            dma((4, 8)),
            dma((4, 8)),
            dma((8,)),
            dma((SWEEPS, 8)),
            dma((GZ - 1,)),
            dma((SWEEPS, GZ - 1)),
            dma((n_plane,)),
            dma((SWEEPS, n_plane)),
        ],
        compiler_params=pltpu.CompilerParams(collective_id=0, has_side_effects=True),
        name="schwarz",
    )(
        well_cells.reshape(-1),
        well_index.reshape(-1),
        rhs,
        start,
        trans,
        accum,
        coupling.reshape((9,) + accum.shape),
        agg_map,
        tile_factors.reshape(72, TILE, TILE),
        coarse_inverse,
    )


def solution(mesh):
    sizes = (mesh.shape["wide"], mesh.shape["narrow"])
    return jax.shard_map(
        functools.partial(per_device, sizes),
        mesh=mesh,
        in_specs=(
            P(None, "wide", "narrow", None),
            P(None, "wide", "narrow", None),
            P(None, "wide", "narrow", None),
            P("wide", "narrow", None),
            P(None, None, "wide", "narrow", None),
            P("wide", "narrow", None),
            P("wide", "narrow", None),
            P("wide", "narrow", None),
            P("wide", "narrow", None, None),
            P(("wide", "narrow"), None),
        ),
        out_specs=(P(None, "wide", "narrow", None), P(None, "wide", "narrow", None)),
        check_vma=False,
    )
```

time: 372 us -> 65.9 us (0.18); the launches traced: 365 us -> 65.7 us
  blocking collectives: 235 us -> 0 us
  Pallas kernels: 0 us -> 62.2 us
  starting transfers between devices: 51.3 us -> 0 us
  matrix products: 25.2 us -> 0 us
  waiting for transfers between devices: 19.1 us -> 0 us
  local copies, waits for them, and re-layouts: 19.3 us -> 2.84 us
  other arithmetic: 12.4 us -> 0 us
    unnamed x3 -> x0, blocking collectives: 235 us -> none
    pallas_call x0 -> x1, Pallas kernels: none -> 62.2 us  [per_device(): pl.pallas_call(functools.partial(kernel, sizes), out_shape=(shape, shape)...]
    ppermute x20 -> x0, starting transfers between devices: 51.3 us -> none  [the longest x10 39 us: padded(): lax.ppermute(head, axis, [((i + 1) % count, i) for i in range(count)])]
    dot_general x18 -> x0, matrix products: 25.2 us -> none  [the longest x9 16.1 us: tile_apply(): jnp.einsum('cpyj,pykj->cpyk', scaled, factors, preferred_element_type=jnp...]
    ppermute x20 -> x0, waiting for transfers between devices: 19.1 us -> none  [the longest x10 9.95 us: padded(): lax.ppermute(head, axis, [((i + 1) % count, i) for i in range(count)])]
    unnamed x100 -> x2, local copies, waits for them, and re-layouts: 10.3 us -> 2.84 us
    slice x47 -> x0, local copies, waits for them, and re-layouts: 7.07 us -> none  [the longest x6 3.55 us: east_of(): return jnp.concatenate([values[..., middle:], from_next], axis=-1)]
    sub x3 -> x0, other arithmetic: 4.27 us -> none  [extended_fn(): extended = (rim_full[13:] - applied)[..., 1:-1, 1:-1, :]]
  transfers between devices with their start and end apart: 20 -> 0, of which waited for: 13 -> 0; matrix products, arithmetic and copies ran while one was open for 1% -> 0% of each run, Pallas kernels for 0% -> 0%
where the time goes in v1:
time: 65.9 us; the launch traced here: 65.7 us
  Pallas kernels  62.2 us (94%)
  local copies, waits for them, and re-layouts  2.84 us (4%)
    pallas_call x1, Pallas kernels, per_device(): pl.pallas_call(functools.partial(kernel, sizes), out_shape=(shape, shape)...  62.2 us
    unnamed x2, local copies, waits for them, and re-layouts  2.84 us

profile of v1, /device:TPU:1, one launch (start us, length us, event | category | flops | bytes accessed | tf_op | source)
XLA Modules:
  0.0 65.7 jit_solution(13220360843176535629)
XLA Ops:
  0.6 62.2 %schwarz.1 = (f32[3,4,8,128]{3,2,1,0:T(8,128)}, f32[3,4,8,128]{3,2,1,0:T(8,128)}) custom-call(s32[64]{0:T(128)} %bitcast.6, f32[64]{0:T(128)} %bitcast.7, f32[3,4,8,128]{3,2,1,0:T(8,128)} %rhs.1, f32[3,4,8,128]{3,2,1,0:T(8,128)} %start.1, f32[3,4,8,128]{3,2,1,0:T(8,128)} %trans.1, f32[4,8,128]{2,1,0:T(8,128)} %accum.1, f32[9,4,8,128]{3,2,1,0:T(8,128)} %bitcast.5, ...), custom_call_target="tpu_custom_call" | custom-call | tf_op jit(solution)/shard_map/schwarz/pallas_call | solution.py:346
  62.8 1.4 %copy.14 = f32[3,4,8,128]{3,2,1,0:T(8,128)} copy(f32[3,4,8,128]{3,2,1,0:T(8,128)} %get-tuple-element.4) | data formatting | bytes 98304
  64.2 1.4 %copy.15 = f32[3,4,8,128]{3,2,1,0:T(8,128)} copy(f32[3,4,8,128]{3,2,1,0:T(8,128)} %get-tuple-element.5) | data formatting | bytes 98304

commit v2 on v1

--- a/solution.py
+++ b/solution.py
@@ -35,7 +35,7 @@
 
 def kernel(
     sizes, cells, wells, rhs, start, trans, accum, coupling, agg, factors, inverse, out_it, out_res,
-    cur, trn, blk, aggx, fac, fct, cinv, cof, own, idx, mis, upd, ybuf, zrec, tbuf, prec, outb,
+    cur, trn, blk, aggx, fac, fct, cinv, cof, own, idx, mis, upd, ybuf, zrec, tbuf, prec,
     lsem, bsem, gsend, grecv, hsend, hrecv, zsend, zrecv, psend, precv,
 ):
     n_wide, n_narrow = sizes
@@ -81,18 +81,8 @@
     load_c = load(inverse, cinv, 6)
     load_f = load(factors, fac, 7)
     upd[...] = jnp.zeros_like(upd)
-    for cp in loads:
+    for cp in loads[:2]:
         cp.wait()
-
-    base = lax.broadcasted_iota(jnp.int32, (PX, CY, TILE), 0) * (CY * TILE)
-    base = base + lax.broadcasted_iota(jnp.int32, (PX, CY, TILE), 1) * TILE
-    base = base + lax.broadcasted_iota(jnp.int32, (PX, CY, TILE), 2)
-
-    def well(n, a):
-        return a + jnp.where(base == cells[n], wells[n], 0.0)
-
-    blk[0, 2:6, 8:16] = lax.fori_loop(0, cells.shape[0], well, blk[0, 2:6, 8:16])
-
     pl.semaphore_wait(bar, len(peers))
 
     def halo(ref, lead, rim, ssem, rsem):
@@ -117,24 +107,39 @@
     h_trn = halo(trn, (every,), (2, 3), gsend.at[1], grecv.at[1])
     h_blk = halo(blk, (every,), (1, 2), gsend.at[2], grecv.at[2])
     h_agg = halo(aggx, (), (2, 3), gsend.at[3], grecv.at[3])
-    for group in (h_cur, h_trn, h_blk, h_agg):
-        for cp in group:
-            cp.start()
+    first = h_cur[:4] + [h_trn[0], h_trn[2]]
+    later = h_cur[4:] + [h_trn[1]] + h_trn[3:] + h_blk + h_agg
+    for cp in first:
+        cp.start()
+
+    for cp in loads[2:]:
+        cp.wait()
+    base = lax.broadcasted_iota(jnp.int32, (PX, CY, TILE), 0) * (CY * TILE)
+    base = base + lax.broadcasted_iota(jnp.int32, (PX, CY, TILE), 1) * TILE
+    base = base + lax.broadcasted_iota(jnp.int32, (PX, CY, TILE), 2)
+
+    def well(n, a):
+        return a + jnp.where(base == cells[n], wells[n], 0.0)
+
+    blk[0, 2:6, 8:16] = lax.fori_loop(0, cells.shape[0], well, blk[0, 2:6, 8:16])
+    for cp in later:
+        cp.start()
 
     load_f.wait()
 
     def flip(t, c):
-        fct[pl.ds(pl.multiple_of(t * TILE, TILE), TILE), :] = fac[t].T
+        for u in range(4):
+            fct[pl.ds(pl.multiple_of((4 * t + u) * TILE, TILE), TILE), :] = fac[4 * t + u].T
         return c
 
-    lax.fori_loop(0, fac.shape[0], flip, 0)
+    lax.fori_loop(0, fac.shape[0] // 4, flip, 0)
     load_c.wait()
 
     lane8 = lax.broadcasted_iota(jnp.int32, (CY, TILE), 1)
     lane16 = lax.broadcasted_iota(jnp.int32, (WIN, TILE), 1)
     row16 = lax.broadcasted_iota(jnp.int32, (WIN, TILE), 0)
 
-    for cp in h_cur + h_trn:
+    for cp in first:
         cp.wait_recv()
 
     for p in range(PX):
@@ -167,9 +172,9 @@
         return res
 
     def prepare():
-        for cp in h_blk + h_agg:
+        for cp in later:
             cp.wait_recv()
-        for cp in h_cur + h_trn + h_blk + h_agg:
+        for cp in first + later:
             cp.wait_send()
 
         def one(p, c):
@@ -253,25 +258,23 @@
         def solve(n, c):
             now = lax.rem(n, 2)
 
-            def two(g, cc):
-                for p in (1 + 2 * g, 2 + 2 * g):
-                    res = operate(upd, (now,), p, lambda b: mis[b, p])
-                    q = [cof[4 + b, p] * res[b] for b in range(3)]
-                    cols = []
-                    for t in range(CY + 4):
-                        cols.append(
-                            jnp.concatenate([jnp.where(row16 == t + 1, v, 0.0).astype(BF16) for v in q], axis=0)
-                        )
-                    lhs = jnp.concatenate(cols, axis=1)
-                    depth = (CY + 4) * TILE
-                    f = fct[pl.ds(pl.multiple_of((p - 1) * depth, depth), depth), :]
-                    r = jnp.dot(lhs, f, preferred_element_type=F32)
-                    for b in range(3):
-                        w = pl.ds(ROW0, WIN)
-                        upd[1 - now, b, p, w] = upd[now, b, p, w] + r[b * WIN : (b + 1) * WIN]
-                return cc
-
-            lax.fori_loop(0, 3, two, 0)
+
+            qs = {}
+            for p in range(1, 7):
+                res = operate(upd, (now,), p, lambda b: mis[b, p])
+                qs[p] = [cof[4 + b, p] * res[b] for b in range(3)]
+            for p in range(1, 7):
+                cols = []
+                for t in range(CY + 4):
+                    cols.append(
+                        jnp.concatenate([jnp.where(row16 == t + 1, v, 0.0).astype(BF16) for v in qs[p]], axis=0)
+                    )
+                lhs = jnp.concatenate(cols, axis=1)
+                depth = (CY + 4) * TILE
+                r = jnp.dot(lhs, fct[(p - 1) * depth : p * depth, :], preferred_element_type=F32)
+                for b in range(3):
+                    w = pl.ds(ROW0, WIN)
+                    upd[1 - now, b, p, w] = upd[now, b, p, w] + r[b * WIN : (b + 1) * WIN]
             return c
 
         lax.fori_loop(0, INNER, solve, 0)
@@ -325,12 +328,17 @@
     lax.fori_loop(0, SWEEPS, sweep, 0)
     for p in range(PX):
         for b, v in enumerate(own_misfit(SWEEPS, (0, 1, 2), p)):
-            outb[b, p] = v
-    stores = [
-        load(cur.at[SWEEPS, :, op, orow], out_it, 0),
-        load(outb, out_res, 1),
-    ]
-    for cp in stores:
+            out_res[b, p] = v
+    for b in range(3):
+        for p in range(PX):
+            out_it[b, p] = cur[SWEEPS, b, 2 + p, 8:16]
+
+
+def put(a, b, out_a, out_b, sem):
+    cps = [pltpu.make_async_copy(a, out_a, sem.at[0]), pltpu.make_async_copy(b, out_b, sem.at[1])]
+    for cp in cps:
+        cp.start()
+    for cp in cps:
         cp.wait()
 
 
@@ -341,13 +349,14 @@
     dma = pltpu.SemaphoreType.DMA
     anys = pl.BlockSpec(memory_space=pl.ANY)
     smem = pl.BlockSpec(memory_space=pltpu.SMEM)
+    vmem = pl.BlockSpec(memory_space=pltpu.VMEM)
     n_plane = GY * GX * n_narrow - 1
     shape = jax.ShapeDtypeStruct(rhs.shape, F32)
-    return pl.pallas_call(
+    got = pl.pallas_call(
         functools.partial(kernel, sizes),
-        out_shape=(shape, shape),
+        out_shape=(pltpu.VMEM(rhs.shape, F32),) * 2,
         in_specs=[smem, smem] + [anys] * 8,
-        out_specs=(anys, anys),
+        out_specs=(vmem, vmem),
         scratch_shapes=[
             ext(SWEEPS + 1, 3),
             ext(3),
@@ -365,7 +374,6 @@
             pltpu.VMEM((SWEEPS, GZ - 1, GY, GX + 2, 1, TILE), F32),
             pltpu.VMEM((GY, GX + 2, 1, TILE), F32),
             pltpu.VMEM((SWEEPS, n_plane, 3, 1, TILE), F32),
-            pltpu.VMEM(rhs.shape, F32),
             dma((8,)),
             dma((1,)),
             dma((4, 8)),
@@ -391,6 +399,15 @@
         tile_factors.reshape(72, TILE, TILE),
         coarse_inverse,
     )
+    return pl.pallas_call(
+        put,
+        out_shape=(shape, shape),
+        in_specs=[vmem, vmem],
+        out_specs=(anys, anys),
+        scratch_shapes=[dma((2,))],
+        compiler_params=pltpu.CompilerParams(vmem_limit_bytes=2**20),
+        name="put",
+    )(*got)
 
 
 def solution(mesh):

time: 65.9 us -> 55.8 us (0.85)
  Pallas kernels: 62.2 us -> 55.1 us
  local copies, waits for them, and re-layouts: 2.84 us -> 0 us
    pallas_call x1 -> x2, Pallas kernels: 62.2 us -> 55.1 us  [the longest x1 54.5 us: per_device(): pl.pallas_call(functools.partial(kernel, sizes), out_shape=(pltpu.VMEM(rh...]
    unnamed x2 -> x0, local copies, waits for them, and re-layouts: 2.84 us -> none
where the time goes in v2:
time: 55.8 us
  Pallas kernels  55.1 us (99%)
  between operations  0.64 us (1%)
    pallas_call x1, Pallas kernels, per_device(): pl.pallas_call(functools.partial(kernel, sizes), out_shape=(pltpu.VMEM(rh...  54.5 us

profile of v2, /device:TPU:1, one launch (start us, length us, event | category | flops | bytes accessed | tf_op | source)
XLA Modules:
  0.0 55.8 jit_solution(2334772319974564536)
XLA Ops:
  0.6 54.5 %schwarz.1 = (f32[3,4,8,128]{3,2,1,0:T(8,128)S(1)}, f32[3,4,8,128]{3,2,1,0:T(8,128)S(1)}) custom-call(s32[64]{0:T(128)} %bitcast.6, f32[64]{0:T(128)} %bitcast.7, f32[3,4,8,128]{3,2,1,0:T(8,128)} %rhs.1, f32[3,4,8,128]{3,2,1,0:T(8,128)} %start.1, f32[3,4,8,128]{3,2,1,0:T(8,128)} %trans.1, f32[4,8,128]{2,1,0:T(8,128)} %accum.1, f32[9,4,8,128]{3,2,1,0:T(8,128)} %bitcast.5, ...), custom_call_target="tpu_custom_call" | custom-call | tf_op jit(solution)/shard_map/schwarz/pallas_call | solution.py:355
  55.1 0.7 %put.1 = (f32[3,4,8,128]{3,2,1,0:T(8,128)}, f32[3,4,8,128]{3,2,1,0:T(8,128)}) custom-call(f32[3,4,8,128]{3,2,1,0:T(8,128)S(1)} %get-tuple-element.4.a, f32[3,4,8,128]{3,2,1,0:T(8,128)S(1)} %get-tuple-element.5.b), custom_call_target="tpu_custom_call" | custom-call | tf_op jit(solution)/shard_map/put/pallas_call | solution.py:402
